TPU v7x, 32 devices: a whole 2x2x4 slice. The times are simulated.
32 devices in a mesh: dp: 2 (over x), col: 4 (over z), row: 4 (over y, core).
Axes of the slice: x: 2, y: 2, z: 4, core: 2. Of those that a mesh axis runs over, the one named last changes fastest.
Arguments:
- x_in: bfloat16 [2, 2048, 6144], P(None, ('dp', 'row'), 'col'), parts along dimension 1
- ln_gamma: float32 [6144], P('col')
- w_in: bfloat16 [6144, 24576], P('row', 'col')
- w_out: bfloat16 [24576, 6144], P('row', 'col')
Outputs:
- output: bfloat16 [2, 2048, 6144], P(None, ('dp', 'row'), 'col'), parts along dimension 1
There are 2 independent parts. A program takes and returns all parts, laid end to end along the dimension named above; an argument that names none is the same for every part.
All inputs are finite; a program needn't handle non-finite values.
Results may differ from a plain program's by a relative error of at most 0.001.
Values are sent between devices in bfloat16 or wider.
A program may use at most 1 GiB of HBM per device.

v0:
```python
import jax
import jax.numpy as jnp
from jax import lax
from jax.sharding import PartitionSpec as P

LN_EPS = 1e-5


def solution(mesh):
    col_size = mesh.shape["col"]
    act_spec = P(None, ("dp", "row"), "col")

    def per_device(x_blk, gamma_blk, w_in_blk, w_out_blk):
        d_model = gamma_blk.shape[0] * col_size
        x_f32 = x_blk.astype(jnp.float32)
        row_stats = jnp.stack([jnp.sum(x_f32, axis=-1), jnp.sum(x_f32 * x_f32, axis=-1)])
        row_stats = lax.psum(row_stats, "col")
        row_mean = row_stats[0] / d_model
        row_var = row_stats[1] / d_model - row_mean * row_mean
        inv_std = lax.rsqrt(row_var + LN_EPS)
        z_norm = ((x_f32 - row_mean[..., None]) * inv_std[..., None] * gamma_blk).astype(jnp.bfloat16)
        z_panel = lax.all_gather(z_norm, "col", axis=2, tiled=True)
        w_in_panel = lax.all_gather(w_in_blk, "row", axis=0, tiled=True)
        hidden = jnp.dot(z_panel, w_in_panel, preferred_element_type=jnp.float32)
        hidden = jax.nn.gelu(hidden, approximate=True).astype(jnp.bfloat16)
        h_panel = lax.all_gather(hidden, "col", axis=2, tiled=True)
        w_out_panel = lax.all_gather(w_out_blk, "row", axis=0, tiled=True)
        branch = jnp.dot(h_panel, w_out_panel, preferred_element_type=jnp.float32)
        return (x_f32 + branch).astype(jnp.bfloat16)

    return jax.shard_map(per_device, mesh=mesh, in_specs=(act_spec, P("col"), P("row", "col"), P("row", "col")), out_specs=act_spec, check_vma=False)
```

profile of v0, /device:TPU:0, one launch (start us, length us, event | category | flops | bytes accessed | tf_op | source)
XLA Modules:
  0.0 1503.6 jit_solution(5324700429487741619)
XLA Ops:
  6.5 0.0 all-gather.5.cloned.1.call-start
  6.5 2.0 convert_reduce_fusion
  8.5 13.5 psum.7
  22.1 3.1 fusion.19
  25.2 0.0 all-gather.5.cloned.1.call-update
  25.2 0.0 all-gather.7.cloned.1.call-start
  25.2 0.7 all-gather.7.cloned.1.call-update
  25.9 0.0 all-gather.11.cloned.1.call-start
  26.0 0.7 all-gather.11.cloned.1.call-update
  26.7 0.0 copy-start
  26.7 0.0 all-gather.9.cloned.1.call-start
  26.7 111.7 %all-gather.5.cloned.1.call-done = bf16[2,256,6144]{2,1,0:T(8,128)(2,1)} async-done(((bf16[2,256,1536]{2,1,0:T(8,128)(2,1)}), bf16[2,256,6144]{2,1,0:T(8,128)(2,1)}) %all-gather.5.cloned.1.call-update) | async-done | bytes 6291472 | tf_op jit(solution)/shard_map/all_gather | solution.py:22
  138.4 441.3 %all-gather.7.cloned.1.call-done = bf16[6144,6144]{1,0:T(8,128)(2,1)} async-done(((bf16[1536,6144]{1,0:T(8,128)(2,1)}), bf16[6144,6144]{1,0:T(8,128)(2,1)}) %all-gather.7.cloned.1.call-update) | async-done | bytes 75497488 | tf_op jit(solution)/shard_map/all_gather | solution.py:23
  579.7 49.7 %fusion.11 = bf16[2,256,6144]{2,1,0:T(8,128)(2,1)} fusion(bf16[2,256,6144]{2,1,0:T(8,128)(2,1)} %all-gather.5.cloned.1.call-done, bf16[6144,6144]{1,0:T(8,128)(2,1)} %all-gather.7.cloned.1.call-done), kind=kOutput, calls=%fused_computation.12 | convolution fusion | flops 38683017216 | bytes 88080384 | tf_op jit(solution)/shard_map/dot_general | solution.py:24
  629.4 0.0 all-gather.9.cloned.1.call-update
  629.4 393.0 %all-gather.11.cloned.1.call-done = bf16[24576,1536]{1,0:T(8,128)(2,1)} async-done(((bf16[6144,1536]{1,0:T(8,128)(2,1)}), bf16[24576,1536]{1,0:T(8,128)(2,1)}) %all-gather.11.cloned.1.call-update) | async-done | bytes 75497488 | tf_op jit(solution)/shard_map/all_gather | solution.py:27
  1022.4 427.4 %all-gather.9.cloned.1.call-done = bf16[2,256,24576]{2,1,0:T(8,128)(2,1)} async-done(((bf16[2,256,6144]{2,1,0:T(8,128)(2,1)}), bf16[2,256,24576]{2,1,0:T(8,128)(2,1)}) %all-gather.9.cloned.1.call-update) | async-done | bytes 25165840 | tf_op jit(solution)/shard_map/all_gather | solution.py:26
  1449.9 0.0 copy-done
  1449.9 47.2 %fusion.20 = bf16[2,256,1536]{2,1,0:T(8,128)(2,1)} fusion(bf16[2,256,24576]{2,1,0:T(8,128)(2,1)} %all-gather.9.cloned.1.call-done, bf16[24576,1536]{1,0:T(8,128)(2,1)} %all-gather.11.cloned.1.call-done, bf16[2,256,1536]{2,1,0:T(8,128)(2,1)S(1)} %copy-done), kind=kOutput, calls=%fused_computation.21 | convolution fusion | flops 38657064960 | bytes 103809024 | tf_op jit(solution)/shard_map/dot_general | solution.py:28
  (3 shorter events, 0.0 us)
Async XLA Ops:
  6.5 131.9 %all-gather.5.cloned.1.call-start = ((), (), s32[]{:S(2)}) async-start(), calls=%async_computation | async-start | bytes 7864320 | tf_op jit(solution)/shard_map/all_gather | solution.py:22
  25.2 554.5 %all-gather.7.cloned.1.call-start = ((), (), s32[]{:S(2)}) async-start(), calls=%async_computation.1 | async-start | bytes 94371840 | tf_op jit(solution)/shard_map/all_gather | solution.py:23
  25.9 996.5 %all-gather.11.cloned.1.call-start = ((), (), s32[]{:S(2)}) async-start(), calls=%async_computation.3 | async-start | bytes 94371840 | tf_op jit(solution)/shard_map/all_gather | solution.py:27
  26.7 1423.2 %copy-start = (bf16[2,256,1536]{2,1,0:T(8,128)(2,1)S(1)}, bf16[2,256,1536]{2,1,0:T(8,128)(2,1)}, u32[]{:S(2)}) copy-start(bf16[2,256,1536]{2,1,0:T(8,128)(2,1)} %param.4) | copy-start | bytes 4718596
  26.7 1423.2 %all-gather.9.cloned.1.call-start = ((), (), s32[]{:S(2)}) async-start(), calls=%async_computation.2 | async-start | bytes 31457280 | tf_op jit(solution)/shard_map/all_gather | solution.py:26
Sparse Core Ops, SparseCore 0:
  25.3 113.0 all-gather.4
  140.0 439.6 all-gather.6
  581.3 441.1 all-gather.10
  1023.9 425.9 all-gather.8
where the time goes:
time: 1500 us
  waiting for transfers between devices  1370 us (91%)
  matrix products  96.9 us (6%)
    all_gather x1, waiting for transfers between devices, per_device(): w_in_panel = lax.all_gather(w_in_blk, 'row', axis=0, tiled=True)  441 us
    all_gather x1, waiting for transfers between devices, per_device(): h_panel = lax.all_gather(hidden, 'col', axis=2, tiled=True)  427 us
    all_gather x1, waiting for transfers between devices, per_device(): w_out_panel = lax.all_gather(w_out_blk, 'row', axis=0, tiled=True)  393 us
    all_gather x1, waiting for transfers between devices, per_device(): z_panel = lax.all_gather(z_norm, 'col', axis=2, tiled=True)  112 us
    dot_general x1, matrix products, per_device(): hidden = jnp.dot(z_panel, w_in_panel, preferred_element_type=jnp.float32)  49.7 us
    dot_general x1, matrix products, per_device(): branch = jnp.dot(h_panel, w_out_panel, preferred_element_type=jnp.float32)  47.2 us
  transfers between devices with their start and end apart: 4, of which 4 were waited for; matrix products, arithmetic and copies ran while one was open for 3% of the time, Pallas kernels for 0%

commit v1 on v0

v1 whole, which is shorter than its diff:
```python
import functools

import jax
import jax.numpy as jnp
from jax import lax
from jax.experimental import pallas as pl
from jax.experimental.pallas import tpu as pltpu
from jax.sharding import PartitionSpec as P

LN_EPS = 1e-5
MESH = pl.DeviceIdType.MESH
NCHUNK = 6
LN_ROWS = 16


def _kernel(
    x_ref, gamma_ref, w1_ref, w2_ref,
    y_ref, w1g, w2g, hg,
    xg, zv, gg, wbuf, hst, acc, hin, w2in, part, xres,
    ys, yr, xs, xr, ps, pr,
    xsu, xsd, xrecv, xps, xpr, gs, gr, hsu, hsd, hrecv, fs, fr,
    lsem, wsem, hsem, msem,
):
    dp, z, row = lax.axis_index("dp"), lax.axis_index("col"), lax.axis_index("row")
    yy, c = row // 2, row % 2
    tok, dblk = x_ref.shape
    toks = 2 * tok
    rows1, fz = w1_ref.shape
    fhalf = fz // 2
    nc = fhalf // NCHUNK
    half1, half2 = rows1 // 2, nc // 2
    nt = wbuf.shape[2]
    d_model = 4 * dblk

    partner = (dp, z, 2 * yy + (1 - c))
    xnb = (1 - dp, z, row)
    ynb = [(dp, z, 2 * (1 - yy) + ct) for ct in range(2)]
    up = (dp, jnp.minimum(z + 1, 3), row)
    dn = (dp, jnp.maximum(z - 1, 0), row)
    zoth = [(dp, (z + k) % 4, row) for k in range(1, 4)]

    def rcopy(src, dst, ssem, rsem, dev):
        return pltpu.make_async_remote_copy(
            src_ref=src, dst_ref=dst, send_sem=ssem, recv_sem=rsem, device_id=dev, device_id_type=MESH)

    def y_desc(w, j, ct):
        if w == 0:
            src = w1_ref.at[pl.ds(dp * half1, half1), pl.ds(ct * fhalf + j * nc, nc)]
            dst = w1g.at[j, row, pl.ds(dp * half1, half1), :]
        else:
            src = w2_ref.at[pl.ds(ct * fhalf + j * nc + dp * half2, half2), :]
            dst = w2g.at[row, j, pl.ds(dp * half2, half2), :]
        return rcopy(src, dst, ys.at[w, j, ct], yr.at[w, j, c], ynb[ct])

    def region(w, j, cs, side):
        rr = 2 * (1 - yy) + cs
        if w == 0:
            return w1g.at[j, rr, pl.ds(side * half1, half1), :]
        return w2g.at[rr, j, pl.ds(side * half2, half2), :]

    def y_arrive_forward(w, j):
        for cs in range(2):
            reg = region(w, j, cs, dp)
            rcopy(reg, reg, ys.at[w, j, cs], yr.at[w, j, cs], ynb[cs]).wait_recv()
            rcopy(reg, reg, xs.at[w, j, cs], xr.at[w, j, cs], xnb).start()

    def x_arrive(w, j):
        for cs in range(2):
            reg = region(w, j, cs, 1 - dp)
            rcopy(reg, reg, xs.at[w, j, cs], xr.at[w, j, cs], xnb).wait_recv()

    def x_sent(w, j):
        for cs in range(2):
            reg = region(w, j, cs, dp)
            rcopy(reg, reg, xs.at[w, j, cs], xr.at[w, j, cs], xnb).wait_send()

    def p_desc(w, j):
        if w == 0:
            src = w1_ref.at[:, pl.ds((1 - c) * fhalf + j * nc, nc)]
            dst = w1g.at[j, row]
        else:
            src = w2_ref.at[pl.ds((1 - c) * fhalf + j * nc, nc), :]
            dst = w2g.at[row, j]
        return rcopy(src, dst, ps.at[w, j], pr.at[w, j], partner)

    def p_arrive(w, j):
        rp = 2 * yy + (1 - c)
        dst = w1g.at[j, rp] if w == 0 else w2g.at[rp, j]
        rcopy(dst, dst, ps.at[w, j], pr.at[w, j], partner).wait_recv()

    def x_blk(zz):
        return xg.at[zz, pl.ds(c * tok, tok), :]

    def x_up(zz, src=None):
        return rcopy(x_blk(zz) if src is None else src, x_blk(zz), xsu.at[zz], xrecv.at[zz], up)

    def x_dn(zz, src=None):
        return rcopy(x_blk(zz) if src is None else src, x_blk(zz), xsd.at[zz], xrecv.at[zz], dn)

    def x_part(zz, src=None):
        return rcopy(x_blk(zz) if src is None else src, x_blk(zz), xps.at[zz], xpr.at[zz], partner)

    def h_up(zz, j):
        return rcopy(hg.at[zz, j], hg.at[zz, j], hsu.at[zz, j], hrecv.at[zz, j], up)

    def h_dn(zz, j):
        return rcopy(hg.at[zz, j], hg.at[zz, j], hsd.at[zz, j], hrecv.at[zz, j], dn)

    barrier = pltpu.get_barrier_semaphore()
    peers = [partner, xnb] + ynb + zoth
    for dev in peers:
        pl.semaphore_signal(barrier, inc=1, device_id=dev, device_id_type=MESH)
    pl.semaphore_wait(barrier, len(peers))

    @pl.when(z < 3)
    def _():
        x_up(z, x_ref).start()

    @pl.when(z > 0)
    def _():
        x_dn(z, x_ref).start()

    x_part(z, x_ref).start()
    own_x = pltpu.make_async_copy(x_ref, x_blk(z), lsem.at[0])
    own_x.start()
    res_x = pltpu.make_async_copy(x_ref, xres, lsem.at[1])
    res_x.start()
    own_g = pltpu.make_async_copy(gamma_ref, gg.at[z], lsem.at[2])
    own_g.start()
    for k in range(3):
        rcopy(gamma_ref, gg.at[z], gs.at[k], gr.at[z], zoth[k]).start()

    def start_w(w):
        def body(j, _):
            p_desc(w, j).start()
            for ct in range(2):
                y_desc(w, j, ct).start()
            return 0
        lax.fori_loop(0, NCHUNK, body, 0)

    start_w(0)

    def zero(i, _):
        acc[pl.ds(i * 64, 64), :] = jnp.zeros((64, acc.shape[1]), jnp.float32)
        return 0
    lax.fori_loop(0, toks // 64, zero, 0)

    def hop(h, desc_up, desc_dn, extra=None):
        @pl.when(z >= h)
        def _():
            desc_up(z - h).wait_recv()

            @pl.when(z < 3)
            def _():
                desc_up(z - h).start()
            if extra is not None:
                extra(z - h)

        @pl.when(z + h <= 3)
        def _():
            desc_dn(z + h).wait_recv()

            @pl.when(z > 0)
            def _():
                desc_dn(z + h).start()
            if extra is not None:
                extra(z + h)

    for h in (1, 2, 3):
        hop(h, x_up, x_dn, lambda zz: x_part(zz).start())
        y_arrive_forward(0, h - 1)

    for zz in range(4):
        blk = xg.at[zz, pl.ds((1 - c) * tok, tok), :]
        rcopy(blk, blk, xps.at[zz], xpr.at[zz], partner).wait_recv()
    own_x.wait()
    own_g.wait()
    res_x.wait()
    for k in range(3):
        zo = (z + k + 1) % 4
        rcopy(gg.at[zo], gg.at[zo], gs.at[k], gr.at[zo], zoth[k]).wait_recv()

    def norm(i, _):
        rs = pl.ds(pl.multiple_of(i * LN_ROWS, LN_ROWS), LN_ROWS)
        s1 = jnp.zeros((LN_ROWS, 1), jnp.float32)
        s2 = jnp.zeros((LN_ROWS, 1), jnp.float32)
        for q in range(4):
            v = xg[q, rs, :].astype(jnp.float32)
            s1 += jnp.sum(v, axis=-1, keepdims=True)
            s2 += jnp.sum(v * v, axis=-1, keepdims=True)
        mean = s1 / d_model
        inv = lax.rsqrt(s2 / d_model - mean * mean + LN_EPS)
        for q in range(4):
            v = xg[q, rs, :].astype(jnp.float32)
            g = gg[q, 0:1, :]
            zv[rs, q * dblk:(q + 1) * dblk] = ((v - mean) * inv * g).astype(jnp.bfloat16)
        return 0
    lax.fori_loop(0, toks // LN_ROWS, norm, 0)

    start_w(1)

    def w1_loads(j, s):
        out = []
        for k in range(4):
            rr = (row + k) % 4
            dst = wbuf.at[s, pl.ds(rr * rows1, rows1), :]
            if k == 0:
                src = w1_ref.at[:, pl.ds(c * fhalf + j * nc + s * nt, nt)]
            else:
                src = w1g.at[j, rr, :, pl.ds(s * nt, nt)]
            out.append(pltpu.make_async_copy(src, dst, wsem.at[s, k]))
        return out

    def mat1(j, _):
        @pl.when(j == 3)
        def _():
            y_arrive_forward(0, 3)
            y_arrive_forward(0, 4)

        @pl.when(j == 4)
        def _():
            y_arrive_forward(0, 5)

        p_arrive(0, j)
        x_arrive(0, j)
        for s in range(nc // nt):
            for cp in w1_loads(j, s):
                cp.start()
        for s in range(nc // nt):
            for cp in w1_loads(j, s):
                cp.wait()

            def mtile(m, _):
                ms = pl.ds(pl.multiple_of(m * 512, 512), 512)
                u = jnp.dot(zv[ms, :], wbuf[s], preferred_element_type=jnp.float32)
                hst[ms, s * nt:(s + 1) * nt] = jax.nn.gelu(u, approximate=True).astype(jnp.bfloat16)
                return 0
            lax.fori_loop(0, toks // 512, mtile, 0)
        st = pltpu.make_async_copy(hst, hg.at[z, j], hsem.at[0])
        st.start()
        st.wait()

        @pl.when(z < 3)
        def _():
            h_up(z, j).start()

        @pl.when(z > 0)
        def _():
            h_dn(z, j).start()
        return 0
    lax.fori_loop(0, NCHUNK, mat1, 0)

    def w2_load(zz, j, s):
        dst = w2in.at[s]

        @pl.when(zz == row)
        def _():
            pltpu.make_async_copy(w2_ref.at[pl.ds(c * fhalf + j * nc, nc), :], dst, msem.at[s, 0]).start()

        @pl.when(zz != row)
        def _():
            pltpu.make_async_copy(w2g.at[zz, j], dst, msem.at[s, 0]).start()

    def mat2(pair, j):
        for s in range(2):
            w2_load(pair[s], j, s)
            pltpu.make_async_copy(hg.at[pair[s], j], hin.at[s], msem.at[s, 1]).start()
        for s in range(2):
            pltpu.make_async_copy(w2g.at[pair[s], j], w2in.at[s], msem.at[s, 0]).wait()
            pltpu.make_async_copy(hg.at[pair[s], j], hin.at[s], msem.at[s, 1]).wait()

            def mtile(m, _):
                ms = pl.ds(pl.multiple_of(m * 256, 256), 256)
                acc[ms, :] += jnp.dot(hin[s, ms, :], w2in[s], preferred_element_type=jnp.float32)
                return 0
            lax.fori_loop(0, toks // 256, mtile, 0)

    pair_a = (z, z + 1 - 2 * (z % 2))
    zb = (z + 2) % 4
    pair_b = (zb, zb + 1 - 2 * (zb % 2))

    def b1(j, _):
        hop(1, lambda zz: h_up(zz, j), lambda zz: h_dn(zz, j))
        return 0
    lax.fori_loop(0, NCHUNK, b1, 0)
    y_arrive_forward(1, 0)

    def b2(j, _):
        hop(2, lambda zz: h_up(zz, j), lambda zz: h_dn(zz, j))

        @pl.when(j < NCHUNK - 1)
        def _():
            y_arrive_forward(1, jnp.minimum(j + 1, NCHUNK - 1))
        p_arrive(1, j)
        x_arrive(1, j)
        mat2(pair_a, j)
        return 0
    lax.fori_loop(0, NCHUNK, b2, 0)

    def b3(j, _):
        hop(3, lambda zz: h_up(zz, j), lambda zz: h_dn(zz, j))
        mat2(pair_b, j)
        return 0
    lax.fori_loop(0, NCHUNK, b3, 0)

    fin = rcopy(acc.at[pl.ds((1 - c) * tok, tok), :], part, fs, fr, partner)
    fin.start()
    fin.wait()

    def final(i, _):
        rs = pl.ds(pl.multiple_of(i * 64, 64), 64)
        own = acc[pl.ds(pl.multiple_of(c * tok + i * 64, 64), 64), :]
        y_ref[rs, :] = (xres[rs, :].astype(jnp.float32) + (own + part[rs, :])).astype(jnp.bfloat16)
        return 0
    lax.fori_loop(0, tok // 64, final, 0)

    for w in range(2):
        def drain(j, _):
            p_desc(w, j).wait_send()
            for ct in range(2):
                y_desc(w, j, ct).wait_send()
            x_sent(w, j)
            return 0
        lax.fori_loop(0, NCHUNK, drain, 0)
    for k in range(3):
        rcopy(gamma_ref, gg.at[z], gs.at[k], gr.at[z], zoth[k]).wait_send()

    def drain_z(zz, _):
        x_part(zz).wait_send()

        @pl.when(jnp.logical_and(zz <= z, z < 3))
        def _():
            x_up(zz).wait_send()

            def d(j, _):
                h_up(zz, j).wait_send()
                return 0
            lax.fori_loop(0, NCHUNK, d, 0)

        @pl.when(jnp.logical_and(zz >= z, z > 0))
        def _():
            x_dn(zz).wait_send()

            def d(j, _):
                h_dn(zz, j).wait_send()
                return 0
            lax.fori_loop(0, NCHUNK, d, 0)
        return 0
    lax.fori_loop(0, 4, drain_z, 0)


def solution(mesh):
    act_spec = P(None, ("dp", "row"), "col")

    def per_device(x_blk, gamma_blk, w_in_blk, w_out_blk):
        mb, rows, dblk = x_blk.shape
        tok = mb * rows
        fz = w_in_blk.shape[1]
        fhalf = fz // 2
        nc = fhalf // NCHUNK
        bf16, f32 = jnp.bfloat16, jnp.float32
        x2 = x_blk.reshape(tok, dblk)
        g2 = jnp.broadcast_to(gamma_blk[None, :], (8, dblk))
        dma = pltpu.SemaphoreType.DMA
        anyspec = pl.BlockSpec(memory_space=pl.ANY)
        out = pl.pallas_call(
            _kernel,
            out_shape=(
                jax.ShapeDtypeStruct((tok, dblk), bf16),
                jax.ShapeDtypeStruct((NCHUNK, 4, w_in_blk.shape[0], nc), bf16),
                jax.ShapeDtypeStruct((4, NCHUNK, nc, dblk), bf16),
                jax.ShapeDtypeStruct((4, NCHUNK, 2 * tok, nc), bf16),
            ),
            in_specs=[anyspec] * 4,
            out_specs=(pl.BlockSpec(memory_space=pltpu.VMEM), anyspec, anyspec, anyspec),
            scratch_shapes=[
                pltpu.VMEM((4, 2 * tok, dblk), bf16),
                pltpu.VMEM((2 * tok, 4 * dblk), bf16),
                pltpu.VMEM((4, 8, dblk), f32),
                pltpu.VMEM((2, 4 * dblk, 256), bf16),
                pltpu.VMEM((2 * tok, nc), bf16),
                pltpu.VMEM((2 * tok, dblk), f32),
                pltpu.VMEM((2, 2 * tok, nc), bf16),
                pltpu.VMEM((2, nc, dblk), bf16),
                pltpu.VMEM((tok, dblk), f32),
                pltpu.VMEM((tok, dblk), bf16),
                dma((2, NCHUNK, 2)), dma((2, NCHUNK, 2)), dma((2, NCHUNK, 2)), dma((2, NCHUNK, 2)),
                dma((2, NCHUNK)), dma((2, NCHUNK)),
                dma((4,)), dma((4,)), dma((4,)), dma((4,)), dma((4,)), dma((3,)), dma((4,)),
                dma((4, NCHUNK)), dma((4, NCHUNK)), dma((4, NCHUNK)), dma, dma,
                dma((3,)), dma((2, 4)), dma((1,)), dma((2, 2)),
            ],
            compiler_params=pltpu.CompilerParams(
                collective_id=0, has_side_effects=True, vmem_limit_bytes=66_000_000),
            name="mlp",
        )(x2, g2, w_in_blk, w_out_blk)
        return out[0].reshape(mb, rows, dblk)

    return jax.shard_map(
        per_device, mesh=mesh, in_specs=(act_spec, P("col"), P("row", "col"), P("row", "col")),
        out_specs=act_spec, check_vma=False)
```

time: 1500 us -> 582 us (0.39)
  waiting for transfers between devices: 1370 us -> 0 us
  Pallas kernels: 0 us -> 577 us
  matrix products: 96.9 us -> 0 us
    all_gather x4 -> x0, waiting for transfers between devices: 1370 us -> none  [the longest x1 441 us: per_device(): w_in_panel = lax.all_gather(w_in_blk, 'row', axis=0, tiled=True)]
    pallas_call x0 -> x1, Pallas kernels: none -> 577 us  [per_device(): pl.pallas_call(_kernel, out_shape=(jax.ShapeDtypeStruct((tok, dblk), bf16...]
    dot_general x2 -> x0, matrix products: 96.9 us -> none  [the longest x1 49.7 us: per_device(): hidden = jnp.dot(z_panel, w_in_panel, preferred_element_type=jnp.float32)]
  transfers between devices with their start and end apart: 4 -> 0, of which waited for: 4 -> 0; matrix products, arithmetic and copies ran while one was open for 3% -> 0% of each run, Pallas kernels for 0% -> 0%
where the time goes in v1:
time: 582 us; the launch traced here: 581 us
  Pallas kernels  577 us (99%)
    pallas_call x1, Pallas kernels, per_device(): pl.pallas_call(_kernel, out_shape=(jax.ShapeDtypeStruct((tok, dblk), bf16...  577 us

profile of v1, /device:TPU:0, one launch (start us, length us, event | category | flops | bytes accessed | tf_op | source)
XLA Modules:
  0.0 581.3 jit_solution(247689111921703075)
XLA Ops:
  0.0 1.3 broadcast_in_dim.2.gamma_ref
  1.3 577.3 %mlp.1 = (bf16[512,1536]{1,0:T(8,128)(2,1)}, bf16[6,4,1536,512]{3,2,1,0:T(8,128)(2,1)}, bf16[4,6,512,1536]{3,2,1,0:T(8,128)(2,1)}, bf16[4,6,1024,512]{3,2,1,0:T(8,128)(2,1)}) custom-call(bf16[512,1536]{1,0:T(8,128)(2,1)} %bitcast.3, f32[8,1536]{1,0:T(8,128)} %broadcast_in_dim.2.gamma_ref, bf16[1536,6144]{1,0:T(8,128)(2,1)} %w1_ref.1, bf16[6144,1536]{1,0:T(8,128)(2,1)} %w2_ref.1), custom_call_target="tpu_custom_call" | custom-call | tf_op jit(solution)/shard_map/mlp/pallas_call | solution.py:366
  578.7 2.7 copy.6

commit v2 on v1

v2 whole, which is shorter than its diff:
```python
import functools

import jax
import jax.numpy as jnp
from jax import lax
from jax.experimental import pallas as pl
from jax.experimental.pallas import tpu as pltpu
from jax.sharding import PartitionSpec as P

LN_EPS = 1e-5
MESH = pl.DeviceIdType.MESH
NCHUNK = 6
LN_ROWS = 16


def _kernel(
    x_ref, gamma_ref, w1_ref, w2_ref,
    y_ref, w1g, w2g, hg, w2x,
    xg, zv, gg, wbuf, hst, acc, accx, hin, w2in, part, partx, parte, xres,
    ys, yr, xs, xr, ps, pr,
    xsu, xsd, xrecv, xps, xpr, gs, gr, hsu, hsd, hrecv, fs, fr,
    wxs, wxr, pxs, pxr, pes, per,
    lsem, wsem, hsem, msem,
):
    dp, z, row = lax.axis_index("dp"), lax.axis_index("col"), lax.axis_index("row")
    yy, c = row // 2, row % 2
    tok, dblk = x_ref.shape
    toks = 2 * tok
    rows1, fz = w1_ref.shape
    fhalf = fz // 2
    nc = fhalf // NCHUNK
    half1, half2 = rows1 // 2, nc // 2
    nt = wbuf.shape[2]
    d_model = 4 * dblk

    partner = (dp, z, 2 * yy + (1 - c))
    xnb = (1 - dp, z, row)
    ynb = [(dp, z, 2 * (1 - yy) + ct) for ct in range(2)]
    up = (dp, jnp.minimum(z + 1, 3), row)
    dn = (dp, jnp.maximum(z - 1, 0), row)
    zoth = [(dp, (z + k) % 4, row) for k in range(1, 4)]
    zoth2 = [(dp, (z + k) % 4, 2 * yy + (1 - c)) for k in range(1, 4)]
    mbt = tok // 2
    hrow = 2 * mbt
    end = jnp.logical_or(z == 0, z == 3)
    inner = jnp.logical_not(end)
    moved = 1 + yy
    z_in = jnp.where(z < 2, 1, 2)
    z_end = jnp.where(z < 2, 0, 3)

    def rcopy(src, dst, ssem, rsem, dev):
        return pltpu.make_async_remote_copy(
            src_ref=src, dst_ref=dst, send_sem=ssem, recv_sem=rsem, device_id=dev, device_id_type=MESH)

    def y_desc(w, j, ct):
        if w == 0:
            src = w1_ref.at[pl.ds(dp * half1, half1), pl.ds(ct * fhalf + j * nc, nc)]
            dst = w1g.at[j, row, pl.ds(dp * half1, half1), :]
        else:
            src = w2_ref.at[pl.ds(ct * fhalf + j * nc + dp * half2, half2), :]
            dst = w2g.at[row, j, pl.ds(dp * half2, half2), :]
        return rcopy(src, dst, ys.at[w, j, ct], yr.at[w, j, c], ynb[ct])

    def region(w, j, cs, side):
        rr = 2 * (1 - yy) + cs
        if w == 0:
            return w1g.at[j, rr, pl.ds(side * half1, half1), :]
        return w2g.at[rr, j, pl.ds(side * half2, half2), :]

    def y_arrive_forward(w, j):
        for cs in range(2):
            reg = region(w, j, cs, dp)
            rcopy(reg, reg, ys.at[w, j, cs], yr.at[w, j, cs], ynb[cs]).wait_recv()
            rcopy(reg, reg, xs.at[w, j, cs], xr.at[w, j, cs], xnb).start()

    def x_arrive(w, j):
        for cs in range(2):
            reg = region(w, j, cs, 1 - dp)
            rcopy(reg, reg, xs.at[w, j, cs], xr.at[w, j, cs], xnb).wait_recv()

    def x_sent(w, j):
        for cs in range(2):
            reg = region(w, j, cs, dp)
            rcopy(reg, reg, xs.at[w, j, cs], xr.at[w, j, cs], xnb).wait_send()

    def p_desc(w, j):
        if w == 0:
            src = w1_ref.at[:, pl.ds((1 - c) * fhalf + j * nc, nc)]
            dst = w1g.at[j, row]
        else:
            src = w2_ref.at[pl.ds((1 - c) * fhalf + j * nc, nc), :]
            dst = w2g.at[row, j]
        return rcopy(src, dst, ps.at[w, j], pr.at[w, j], partner)

    def p_arrive(w, j):
        rp = 2 * yy + (1 - c)
        dst = w1g.at[j, rp] if w == 0 else w2g.at[rp, j]
        rcopy(dst, dst, ps.at[w, j], pr.at[w, j], partner).wait_recv()

    def x_blk(zz, m):
        return xg.at[zz, pl.ds(m * hrow + c * mbt, mbt), :]

    def x_src(m):
        return x_ref.at[pl.ds(m * mbt, mbt), :]

    def x_up(zz, m, src=None):
        return rcopy(x_blk(zz, m) if src is None else src, x_blk(zz, m), xsu.at[zz, m], xrecv.at[zz, m], up)

    def x_dn(zz, m, src=None):
        return rcopy(x_blk(zz, m) if src is None else src, x_blk(zz, m), xsd.at[zz, m], xrecv.at[zz, m], dn)

    def x_part(zz, m, src=None):
        return rcopy(x_blk(zz, m) if src is None else src, x_blk(zz, m), xps.at[zz, m], xpr.at[zz, m], partner)

    def h_blk(zz, j, m):
        return hg.at[zz, j, pl.ds(m * hrow, hrow), :]

    def h_up(zz, j, m):
        return rcopy(h_blk(zz, j, m), h_blk(zz, j, m), hsu.at[zz, j, m], hrecv.at[zz, j, m], up)

    def h_dn(zz, j, m):
        return rcopy(h_blk(zz, j, m), h_blk(zz, j, m), hsd.at[zz, j, m], hrecv.at[zz, j, m], dn)

    def goes_up(zz):
        return jnp.logical_and(z < 3, jnp.logical_not(jnp.logical_and(z == 2, zz == moved)))

    def goes_dn(zz):
        return jnp.logical_and(z > 0, jnp.logical_not(jnp.logical_and(z == 1, zz == moved)))

    def wx_desc(j, ct):
        return rcopy(w2_ref.at[pl.ds(ct * fhalf + j * nc, nc), :], w2x.at[j], wxs.at[j, ct], wxr.at[j],
                     (dp, z_in, 2 * yy + ct))

    def px_desc(m):
        return rcopy(accx.at[pl.ds(m * hrow + (1 - c) * mbt, mbt), :], partx.at[pl.ds(m * mbt, mbt), :],
                     pxs.at[m], pxr.at[m], partner)

    def pe_desc():
        return rcopy(partx, parte, pes, per, (dp, z_end, row))

    barrier = pltpu.get_barrier_semaphore()
    peers = [partner, xnb] + ynb + zoth + zoth2
    for dev in peers:
        pl.semaphore_signal(barrier, inc=1, device_id=dev, device_id_type=MESH)
    pl.semaphore_wait(barrier, len(peers))

    def own_x_send(m):
        @pl.when(z < 3)
        def _():
            x_up(z, m, x_src(m)).start()

        @pl.when(z > 0)
        def _():
            x_dn(z, m, x_src(m)).start()

        x_part(z, m, x_src(m)).start()

    own_x_send(0)
    own_x = [pltpu.make_async_copy(x_src(m), x_blk(z, m), lsem.at[m]) for m in range(2)]
    own_x[0].start()
    own_x[1].start()
    res_x = pltpu.make_async_copy(x_ref, xres, lsem.at[2])
    res_x.start()
    own_g = pltpu.make_async_copy(gamma_ref, gg.at[z], lsem.at[3])
    own_g.start()
    for k in range(3):
        rcopy(gamma_ref, gg.at[z], gs.at[k], gr.at[z], zoth[k]).start()

    def start_w(w):
        def body(j, _):
            p_desc(w, j).start()
            for ct in range(2):
                y_desc(w, j, ct).start()
            return 0
        lax.fori_loop(0, NCHUNK, body, 0)

    def start_wx(js):
        @pl.when(jnp.logical_and(end, row == moved))
        def _():
            for j in js:
                for ct in range(2):
                    wx_desc(j, ct).start()

    def zero():
        def body(i, _):
            rs = pl.ds(pl.multiple_of(i * 64, 64), 64)
            acc[rs, :] = jnp.zeros((64, acc.shape[1]), jnp.float32)
            accx[rs, :] = jnp.zeros((64, acc.shape[1]), jnp.float32)
            return 0
        lax.fori_loop(0, toks // 64, body, 0)

    def xhop(h, m):
        @pl.when(z >= h)
        def _():
            x_up(z - h, m).wait_recv()

            @pl.when(z < 3)
            def _():
                x_up(z - h, m).start()
            x_part(z - h, m).start()

        @pl.when(z + h <= 3)
        def _():
            x_dn(z + h, m).wait_recv()

            @pl.when(z > 0)
            def _():
                x_dn(z + h, m).start()
            x_part(z + h, m).start()

    def x_done(m):
        for zz in range(4):
            blk = xg.at[zz, pl.ds(m * hrow + (1 - c) * mbt, mbt), :]
            rcopy(blk, blk, xps.at[zz, m], xpr.at[zz, m], partner).wait_recv()
        own_x[m].wait()

    def gamma_done():
        own_g.wait()
        res_x.wait()
        for k in range(3):
            zo = (z + k + 1) % 4
            rcopy(gg.at[zo], gg.at[zo], gs.at[k], gr.at[zo], zoth[k]).wait_recv()

    def norm(m):
        def body(i, _):
            rs = pl.ds(pl.multiple_of(m * hrow + i * LN_ROWS, LN_ROWS), LN_ROWS)
            s1 = jnp.zeros((LN_ROWS, 1), jnp.float32)
            s2 = jnp.zeros((LN_ROWS, 1), jnp.float32)
            for q in range(4):
                v = xg[q, rs, :].astype(jnp.float32)
                s1 += jnp.sum(v, axis=-1, keepdims=True)
                s2 += jnp.sum(v * v, axis=-1, keepdims=True)
            mean = s1 / d_model
            inv = lax.rsqrt(s2 / d_model - mean * mean + LN_EPS)
            for q in range(4):
                v = xg[q, rs, :].astype(jnp.float32)
                g = gg[q, 0:1, :]
                zv[rs, q * dblk:(q + 1) * dblk] = ((v - mean) * inv * g).astype(jnp.bfloat16)
            return 0
        lax.fori_loop(0, hrow // LN_ROWS, body, 0)

    def w1_loads(j, s):
        out = []
        for k in range(4):
            rr = (row + k) % 4
            dst = wbuf.at[s, pl.ds(rr * rows1, rows1), :]
            if k == 0:
                src = w1_ref.at[:, pl.ds(c * fhalf + j * nc + s * nt, nt)]
            else:
                src = w1g.at[j, rr, :, pl.ds(s * nt, nt)]
            out.append(pltpu.make_async_copy(src, dst, wsem.at[s, k]))
        return out

    ntile = nc // nt

    def w1_ready(j):
        p_arrive(0, j)
        x_arrive(0, j)
        for s in range(ntile):
            for cp in w1_loads(j, s):
                cp.start()

    def mat1(j, lo=0, hi=2):
        for m in range(lo, hi):
            def tile(s, _):
                if m == lo and lo == 0:
                    for cp in w1_loads(j, s):
                        cp.wait()
                u = jnp.dot(zv[m * hrow:(m + 1) * hrow, :], wbuf[s], preferred_element_type=jnp.float32)
                hst[m * hrow:(m + 1) * hrow, pl.ds(pl.multiple_of(s * nt, nt), nt)] = jax.nn.gelu(
                    u, approximate=True).astype(jnp.bfloat16)
                return 0
            lax.fori_loop(0, ntile, tile, 0)
            st = pltpu.make_async_copy(hst.at[pl.ds(m * hrow, hrow), :], h_blk(z, j, m), hsem.at[0])
            st.start()
            st.wait()

            @pl.when(goes_up(z))
            def _():
                h_up(z, j, m).start()

            @pl.when(goes_dn(z))
            def _():
                h_dn(z, j, m).start()

    def hop(h, j, ms=(0, 1)):
        for m in ms:
            @pl.when(jnp.logical_and(z >= h, jnp.logical_not(jnp.logical_and(z == 3, z - h == moved))))
            def _():
                h_up(z - h, j, m).wait_recv()

                @pl.when(goes_up(z - h))
                def _():
                    h_up(z - h, j, m).start()

            @pl.when(jnp.logical_and(z + h <= 3, jnp.logical_not(jnp.logical_and(z == 0, z + h == moved))))
            def _():
                h_dn(z + h, j, m).wait_recv()

                @pl.when(goes_dn(z + h))
                def _():
                    h_dn(z + h, j, m).start()

    def mat2(pair, j):
        def load(s, zz):
            dst = w2in.at[s]

            @pl.when(zz == row)
            def _():
                pltpu.make_async_copy(w2_ref.at[pl.ds(c * fhalf + j * nc, nc), :], dst, msem.at[s, 0]).start()

            @pl.when(zz != row)
            def _():
                pltpu.make_async_copy(w2g.at[zz, j], dst, msem.at[s, 0]).start()
            pltpu.make_async_copy(hg.at[zz, j], hin.at[s], msem.at[s, 1]).start()

        def runs(zz):
            return jnp.logical_not(jnp.logical_and(end, zz == moved))

        for s in range(2):
            @pl.when(runs(pair[s]))
            def _():
                load(s, pair[s])

        def block(s, _):
            zz = jnp.where(s == 0, pair[0], pair[1])

            @pl.when(runs(zz))
            def _():
                pltpu.make_async_copy(w2g.at[zz, j], w2in.at[s], msem.at[s, 0]).wait()
                pltpu.make_async_copy(hg.at[zz, j], hin.at[s], msem.at[s, 1]).wait()

                def mtile(m, _):
                    ms = pl.ds(pl.multiple_of(m * 256, 256), 256)
                    acc[ms, :] += jnp.dot(hin[s, ms, :], w2in[s], preferred_element_type=jnp.float32)
                    return 0
                lax.fori_loop(0, toks // 256, mtile, 0)
            return 0
        lax.fori_loop(0, 2, block, 0)

    pair_a = (z, z + 1 - 2 * (z % 2))
    zb = (z + 2) % 4
    pair_b = (zb, zb + 1 - 2 * (zb % 2))

    def w2_ready(j):
        p_arrive(1, j)
        x_arrive(1, j)

    def mat2x(j):
        @pl.when(inner)
        def _():
            rcopy(w2x.at[j], w2x.at[j], wxs.at[j, 0], wxr.at[j], partner).wait_recv()
            a = pltpu.make_async_copy(w2x.at[j], w2in.at[0], msem.at[0, 0])
            b = pltpu.make_async_copy(hg.at[moved, j], hin.at[0], msem.at[0, 1])
            a.start()
            b.start()
            a.wait()
            b.wait()

            def mtile(m, _):
                ms = pl.ds(pl.multiple_of(m * 256, 256), 256)
                accx[ms, :] += jnp.dot(hin[0, ms, :], w2in[0], preferred_element_type=jnp.float32)
                return 0
            lax.fori_loop(0, toks // 256, mtile, 0)

    def px_start():
        @pl.when(inner)
        def _():
            for m in range(2):
                px_desc(m).start()

    def px_finish():
        @pl.when(inner)
        def _():
            for m in range(2):
                px_desc(m).wait_recv()

                def add(i, _):
                    a = pl.ds(pl.multiple_of(m * hrow + c * mbt + i * 64, 64), 64)
                    b = pl.ds(pl.multiple_of(m * mbt + i * 64, 64), 64)
                    partx[b, :] += accx[a, :]
                    return 0
                lax.fori_loop(0, mbt // 64, add, 0)
            pe_desc().start()

    start_w(0)
    zero()
    xhop(1, 0)
    xhop(2, 0)
    own_x_send(1)
    start_wx((0, 1, 2))
    y_arrive_forward(0, 0)
    xhop(3, 0)
    x_done(0)
    gamma_done()
    norm(0)
    xhop(1, 1)
    y_arrive_forward(0, 1)
    xhop(2, 1)
    w1_ready(0)
    mat1(0, 0, 1)
    xhop(3, 1)
    x_done(1)
    norm(1)
    mat1(0, 1, 2)
    y_arrive_forward(0, 2)
    start_w(1)
    w1_ready(1)
    mat1(1)
    hop(1, 0)
    y_arrive_forward(0, 3)
    w1_ready(2)
    mat1(2)
    start_wx((3,))
    hop(1, 1)
    y_arrive_forward(0, 4)
    w1_ready(3)
    mat1(3)
    start_wx((4,))
    hop(2, 0)
    hop(1, 2)
    y_arrive_forward(0, 5)
    w1_ready(4)
    mat1(4)
    start_wx((5,))
    hop(2, 1)
    w1_ready(5)
    mat1(5)
    hop(1, 3)
    y_arrive_forward(1, 0)
    hop(2, 2)
    y_arrive_forward(1, 1)
    hop(1, 4)
    w2_ready(0)
    mat2(pair_a, 0)
    mat2x(0)
    mat2x(1)
    hop(2, 3)
    y_arrive_forward(1, 2)
    w2_ready(1)
    mat2(pair_a, 1)
    mat2x(2)
    mat2x(3)
    hop(1, 5)
    y_arrive_forward(1, 3)
    w2_ready(2)
    mat2(pair_a, 2)
    mat2x(4)
    hop(2, 4)
    mat2x(5)
    px_start()
    hop(2, 5)
    y_arrive_forward(1, 4)
    px_finish()
    w2_ready(3)
    mat2(pair_a, 3)
    hop(3, 0)
    mat2(pair_b, 0)
    y_arrive_forward(1, 5)
    hop(3, 1)
    mat2(pair_b, 1)
    w2_ready(4)
    mat2(pair_a, 4)
    hop(3, 2)
    mat2(pair_b, 2)
    hop(3, 3)
    mat2(pair_b, 3)
    w2_ready(5)
    mat2(pair_a, 5)
    hop(3, 4)
    mat2(pair_b, 4)
    hop(3, 5)
    mat2(pair_b, 5)
    def fin_desc(m):
        return rcopy(acc.at[pl.ds(m * hrow + (1 - c) * mbt, mbt), :], part.at[pl.ds(m * mbt, mbt), :],
                     fs.at[m], fr.at[m], partner)
    for m in range(2):
        fin_desc(m).start()

    @pl.when(end)
    def _():
        pe_desc().wait_recv()

        def add(i, _):
            for m in range(2):
                a = pl.ds(pl.multiple_of(m * hrow + c * mbt + i * 64, 64), 64)
                b = pl.ds(pl.multiple_of(m * mbt + i * 64, 64), 64)
                acc[a, :] += parte[b, :]
            return 0
        lax.fori_loop(0, mbt // 64, add, 0)

    for m in range(2):
        fin_desc(m).wait()

        def final(i, _):
            a = pl.ds(pl.multiple_of(m * hrow + c * mbt + i * 64, 64), 64)
            b = pl.ds(pl.multiple_of(m * mbt + i * 64, 64), 64)
            y_ref[b, :] = (xres[b, :].astype(jnp.float32) + (acc[a, :] + part[b, :])).astype(jnp.bfloat16)
            return 0
        lax.fori_loop(0, mbt // 64, final, 0)

    for w in range(2):
        def drain(j, _):
            p_desc(w, j).wait_send()
            for ct in range(2):
                y_desc(w, j, ct).wait_send()
            x_sent(w, j)
            return 0
        lax.fori_loop(0, NCHUNK, drain, 0)
    for k in range(3):
        rcopy(gamma_ref, gg.at[z], gs.at[k], gr.at[z], zoth[k]).wait_send()

    def drain_z(zz, _):
        for m in range(2):
            x_part(zz, m).wait_send()

        @pl.when(jnp.logical_and(zz <= z, z < 3))
        def _():
            for m in range(2):
                x_up(zz, m).wait_send()

        @pl.when(jnp.logical_and(zz >= z, z > 0))
        def _():
            for m in range(2):
                x_dn(zz, m).wait_send()

        @pl.when(jnp.logical_and(zz <= z, goes_up(zz)))
        def _():
            def d(j, _):
                for m in range(2):
                    h_up(zz, j, m).wait_send()
                return 0
            lax.fori_loop(0, NCHUNK, d, 0)

        @pl.when(jnp.logical_and(zz >= z, goes_dn(zz)))
        def _():
            def d(j, _):
                for m in range(2):
                    h_dn(zz, j, m).wait_send()
                return 0
            lax.fori_loop(0, NCHUNK, d, 0)
        return 0
    lax.fori_loop(0, 4, drain_z, 0)

    @pl.when(jnp.logical_and(end, row == moved))
    def _():
        def d(j, _):
            for ct in range(2):
                wx_desc(j, ct).wait_send()
            return 0
        lax.fori_loop(0, NCHUNK, d, 0)

    @pl.when(inner)
    def _():
        for m in range(2):
            px_desc(m).wait_send()
        pe_desc().wait_send()


def solution(mesh):
    act_spec = P(None, ("dp", "row"), "col")

    def per_device(x_blk, gamma_blk, w_in_blk, w_out_blk):
        mb, rows, dblk = x_blk.shape
        tok = mb * rows
        fz = w_in_blk.shape[1]
        fhalf = fz // 2
        nc = fhalf // NCHUNK
        bf16, f32 = jnp.bfloat16, jnp.float32
        x2 = x_blk.reshape(tok, dblk)
        g2 = jnp.broadcast_to(gamma_blk[None, :], (8, dblk))
        dma = pltpu.SemaphoreType.DMA
        anyspec = pl.BlockSpec(memory_space=pl.ANY)
        out = pl.pallas_call(
            _kernel,
            out_shape=(
                jax.ShapeDtypeStruct((tok, dblk), bf16),
                jax.ShapeDtypeStruct((NCHUNK, 4, w_in_blk.shape[0], nc), bf16),
                jax.ShapeDtypeStruct((4, NCHUNK, nc, dblk), bf16),
                jax.ShapeDtypeStruct((4, NCHUNK, 2 * tok, nc), bf16),
                jax.ShapeDtypeStruct((NCHUNK, nc, dblk), bf16),
            ),
            in_specs=[anyspec] * 4,
            out_specs=(pl.BlockSpec(memory_space=pltpu.VMEM), anyspec, anyspec, anyspec, anyspec),
            scratch_shapes=[
                pltpu.VMEM((4, 2 * tok, dblk), bf16),
                pltpu.VMEM((2 * tok, 4 * dblk), bf16),
                pltpu.VMEM((4, 8, dblk), f32),
                pltpu.VMEM((2, 4 * dblk, 256), bf16),
                pltpu.VMEM((2 * tok, nc), bf16),
                pltpu.VMEM((2 * tok, dblk), f32),
                pltpu.VMEM((2 * tok, dblk), f32),
                pltpu.VMEM((2, 2 * tok, nc), bf16),
                pltpu.VMEM((2, nc, dblk), bf16),
                pltpu.VMEM((tok, dblk), f32),
                pltpu.VMEM((tok, dblk), f32),
                pltpu.VMEM((tok, dblk), f32),
                pltpu.VMEM((tok, dblk), bf16),
                dma((2, NCHUNK, 2)), dma((2, NCHUNK, 2)), dma((2, NCHUNK, 2)), dma((2, NCHUNK, 2)),
                dma((2, NCHUNK)), dma((2, NCHUNK)),
                dma((4, 2)), dma((4, 2)), dma((4, 2)), dma((4, 2)), dma((4, 2)), dma((3,)), dma((4,)),
                dma((4, NCHUNK, 2)), dma((4, NCHUNK, 2)), dma((4, NCHUNK, 2)), dma((2,)), dma((2,)),
                dma((NCHUNK, 2)), dma((NCHUNK,)), dma((2,)), dma((2,)), dma, dma,
                dma((4,)), dma((2, 4)), dma((1,)), dma((2, 2)),
            ],
            compiler_params=pltpu.CompilerParams(
                collective_id=0, has_side_effects=True, vmem_limit_bytes=66_000_000),
            name="mlp",
        )(x2, g2, w_in_blk, w_out_blk)
        return out[0].reshape(mb, rows, dblk)

    return jax.shard_map(
        per_device, mesh=mesh, in_specs=(act_spec, P("col"), P("row", "col"), P("row", "col")),
        out_specs=act_spec, check_vma=False)
```

time: 582 us -> 519 us (0.89)
  the two profiles are of different devices: /device:TPU:0 before, /device:TPU:30 now
where the time goes in v2:
time: 519 us
  Pallas kernels  515 us (99%)
    pallas_call x1, Pallas kernels, per_device(): pl.pallas_call(_kernel, out_shape=(jax.ShapeDtypeStruct((tok, dblk), bf16...  515 us

profile of v2, /device:TPU:30, one launch (start us, length us, event | category | flops | bytes accessed | tf_op | source)
XLA Modules:
  0.0 518.6 jit_solution(14295256626113746948)
XLA Ops:
  0.0 1.3 broadcast_in_dim.2.gamma_ref
  1.3 514.6 %mlp.1 = (bf16[512,1536]{1,0:T(8,128)(2,1)}, bf16[6,4,1536,512]{3,2,1,0:T(8,128)(2,1)}, bf16[4,6,512,1536]{3,2,1,0:T(8,128)(2,1)}, bf16[4,6,1024,512]{3,2,1,0:T(8,128)(2,1)}, bf16[6,512,1536]{2,1,0:T(8,128)(2,1)}) custom-call(bf16[512,1536]{1,0:T(8,128)(2,1)} %bitcast.3, f32[8,1536]{1,0:T(8,128)} %broadcast_in_dim.2.gamma_ref, bf16[1536,6144]{1,0:T(8,128)(2,1)} %w1_ref.1, ...), custom_call_target="tpu_custom_call" | custom-call | tf_op jit(solution)/shard_map/mlp/pallas_call | solution.py:574
  516.0 2.7 copy.6

commit v3 on v2

--- a/solution.py
+++ b/solution.py
@@ -11,15 +11,29 @@
 MESH = pl.DeviceIdType.MESH
 NCHUNK = 6
 LN_ROWS = 16
+EXTRA = ()
+ORDER = (
+    "own_1", "wx_1", "g", "y_0_0", "wx_0", "x_1_0", "x_2_0", "w_1", "x_1_1", "x_3_0", "p_0", "y_0_1",
+    "xd_0", "ln_0", "x_2_1", "f_0_0_1", "x_3_1", "y_0_2", "xd_1", "ln_1", "f_0_1_2", "p_1", "f_1",
+    "h_1_0_0", "y_0_3", "h_1_0_1", "p_2", "h_2_0_0", "f_2", "h_1_1_0", "wx_3", "h_2_0_1", "y_0_4",
+    "h_1_2_0", "h_1_1_1", "h_1_2_1", "p_3", "f_3", "y_0_5", "q_4", "q_1", "q_3", "p_4", "h_2_1_0",
+    "h_3_0_1", "h_2_2_0", "f_4", "y_1_0", "c_0", "wx_2", "q_0", "h_3_0_0", "q_2", "h_1_3_0", "h_2_1_1",
+    "h_1_3_1", "h_3_1_0", "c_1", "h_1_4_0", "p_5", "f_5", "h_1_4_1", "y_1_1", "h_3_1_1", "r_0",
+    "h_2_3_1", "h_2_3_0", "wx_4", "a_0", "h_3_2_0", "h_2_2_1", "h_2_4_0", "y_1_2", "h_1_5_1", "wx_5",
+    "h_1_5_0", "c_2", "y_1_3", "c_4", "h_3_3_0", "h_3_3_1", "b_0", "h_2_5_1", "r_2", "r_1", "h_3_2_1",
+    "c_3", "a_2", "a_1", "h_2_5_0", "b_2", "h_2_4_1", "c_5", "q_5", "r_3", "y_1_4", "h_3_4_0",
+    "h_3_4_1", "ps", "pf", "a_3", "y_1_5", "r_4", "b_3", "b_4", "h_3_5_1", "a_4", "b_1", "h_3_5_0",
+    "a_5", "r_5", "b_5",
+)
 
 
 def _kernel(
     x_ref, gamma_ref, w1_ref, w2_ref,
-    y_ref, w1g, w2g, hg, w2x,
+    y_ref, w1g, w2g, hg, w2x, w2y,
     xg, zv, gg, wbuf, hst, acc, accx, hin, w2in, part, partx, parte, xres,
     ys, yr, xs, xr, ps, pr,
     xsu, xsd, xrecv, xps, xpr, gs, gr, hsu, hsd, hrecv, fs, fr,
-    wxs, wxr, pxs, pxr, pes, per,
+    wxs, wxr, wx2s, wx2r, pxs, pxr, pes, per,
     lsem, wsem, hsem, msem,
 ):
     dp, z, row = lax.axis_index("dp"), lax.axis_index("col"), lax.axis_index("row")
@@ -47,6 +61,7 @@
     moved = 1 + yy
     z_in = jnp.where(z < 2, 1, 2)
     z_end = jnp.where(z < 2, 0, 3)
+    far = 3 - z_end
 
     def rcopy(src, dst, ssem, rsem, dev):
         return pltpu.make_async_remote_copy(
@@ -121,15 +136,24 @@
     def h_dn(zz, j, m):
         return rcopy(h_blk(zz, j, m), h_blk(zz, j, m), hsd.at[zz, j, m], hrecv.at[zz, j, m], dn)
 
-    def goes_up(zz):
-        return jnp.logical_and(z < 3, jnp.logical_not(jnp.logical_and(z == 2, zz == moved)))
-
-    def goes_dn(zz):
-        return jnp.logical_and(z > 0, jnp.logical_not(jnp.logical_and(z == 1, zz == moved)))
+    def not_taken(e, zz, j):
+        if j in EXTRA:
+            return jnp.logical_or(zz == moved, zz == 3 - e)
+        return zz == moved
+
+    def goes_up(zz, j):
+        return jnp.logical_and(z < 3, jnp.logical_not(jnp.logical_and(z == 2, not_taken(3, zz, j))))
+
+    def goes_dn(zz, j):
+        return jnp.logical_and(z > 0, jnp.logical_not(jnp.logical_and(z == 1, not_taken(0, zz, j))))
 
     def wx_desc(j, ct):
         return rcopy(w2_ref.at[pl.ds(ct * fhalf + j * nc, nc), :], w2x.at[j], wxs.at[j, ct], wxr.at[j],
                      (dp, z_in, 2 * yy + ct))
+
+    def wx2_desc(j, own):
+        src = w2_ref.at[pl.ds(c * fhalf + j * nc, nc), :] if own else w2g.at[far, j]
+        return rcopy(src, w2y.at[EXTRA.index(j)], wx2s.at[EXTRA.index(j)], wx2r.at[EXTRA.index(j)], (dp, z_in, row))
 
     def px_desc(m):
         return rcopy(accx.at[pl.ds(m * hrow + (1 - c) * mbt, mbt), :], partx.at[pl.ds(m * mbt, mbt), :],
@@ -275,29 +299,29 @@
             st.start()
             st.wait()
 
-            @pl.when(goes_up(z))
+            @pl.when(goes_up(z, j))
             def _():
                 h_up(z, j, m).start()
 
-            @pl.when(goes_dn(z))
+            @pl.when(goes_dn(z, j))
             def _():
                 h_dn(z, j, m).start()
 
-    def hop(h, j, ms=(0, 1)):
+    def hop(h, j, *ms):
         for m in ms:
-            @pl.when(jnp.logical_and(z >= h, jnp.logical_not(jnp.logical_and(z == 3, z - h == moved))))
+            @pl.when(jnp.logical_and(z >= h, jnp.logical_not(jnp.logical_and(z == 3, not_taken(3, z - h, j)))))
             def _():
                 h_up(z - h, j, m).wait_recv()
 
-                @pl.when(goes_up(z - h))
+                @pl.when(goes_up(z - h, j))
                 def _():
                     h_up(z - h, j, m).start()
 
-            @pl.when(jnp.logical_and(z + h <= 3, jnp.logical_not(jnp.logical_and(z == 0, z + h == moved))))
+            @pl.when(jnp.logical_and(z + h <= 3, jnp.logical_not(jnp.logical_and(z == 0, not_taken(0, z + h, j)))))
             def _():
                 h_dn(z + h, j, m).wait_recv()
 
-                @pl.when(goes_dn(z + h))
+                @pl.when(goes_dn(z + h, j))
                 def _():
                     h_dn(z + h, j, m).start()
 
@@ -315,7 +339,7 @@
             pltpu.make_async_copy(hg.at[zz, j], hin.at[s], msem.at[s, 1]).start()
 
         def runs(zz):
-            return jnp.logical_not(jnp.logical_and(end, zz == moved))
+            return jnp.logical_not(jnp.logical_and(end, not_taken(z_end, zz, j)))
 
         for s in range(2):
             @pl.when(runs(pair[s]))
@@ -338,12 +362,13 @@
             return 0
         lax.fori_loop(0, 2, block, 0)
 
-    pair_a = (z, z + 1 - 2 * (z % 2))
-    zb = (z + 2) % 4
-    pair_b = (zb, zb + 1 - 2 * (zb % 2))
-
-    def w2_ready(j):
+    pair_a = (2 * yy, 2 * yy + 1)
+    pair_b = (2 - 2 * yy, 3 - 2 * yy)
+
+    def w2_local(j):
         p_arrive(1, j)
+
+    def w2_remote(j):
         x_arrive(1, j)
 
     def mat2x(j):
@@ -363,6 +388,34 @@
                 return 0
             lax.fori_loop(0, toks // 256, mtile, 0)
 
+    def start_wx2(j):
+        @pl.when(jnp.logical_and(end, row == far))
+        def _():
+            wx2_desc(j, True).start()
+
+        @pl.when(jnp.logical_and(end, row != far))
+        def _():
+            wx2_desc(j, False).start()
+
+    def mat2y(j):
+        i = EXTRA.index(j)
+
+        @pl.when(inner)
+        def _():
+            rcopy(w2y.at[i], w2y.at[i], wx2s.at[i], wx2r.at[i], partner).wait_recv()
+            a = pltpu.make_async_copy(w2y.at[i], w2in.at[0], msem.at[0, 0])
+            b = pltpu.make_async_copy(hg.at[far, j], hin.at[0], msem.at[0, 1])
+            a.start()
+            b.start()
+            a.wait()
+            b.wait()
+
+            def mtile(m, _):
+                ms = pl.ds(pl.multiple_of(m * 256, 256), 256)
+                accx[ms, :] += jnp.dot(hin[0, ms, :], w2in[0], preferred_element_type=jnp.float32)
+                return 0
+            lax.fori_loop(0, toks // 256, mtile, 0)
+
     def px_start():
         @pl.when(inner)
         def _():
@@ -385,92 +438,14 @@
 
     start_w(0)
     zero()
-    xhop(1, 0)
-    xhop(2, 0)
-    own_x_send(1)
-    start_wx((0, 1, 2))
-    y_arrive_forward(0, 0)
-    xhop(3, 0)
-    x_done(0)
-    gamma_done()
-    norm(0)
-    xhop(1, 1)
-    y_arrive_forward(0, 1)
-    xhop(2, 1)
-    w1_ready(0)
-    mat1(0, 0, 1)
-    xhop(3, 1)
-    x_done(1)
-    norm(1)
-    mat1(0, 1, 2)
-    y_arrive_forward(0, 2)
-    start_w(1)
-    w1_ready(1)
-    mat1(1)
-    hop(1, 0)
-    y_arrive_forward(0, 3)
-    w1_ready(2)
-    mat1(2)
-    start_wx((3,))
-    hop(1, 1)
-    y_arrive_forward(0, 4)
-    w1_ready(3)
-    mat1(3)
-    start_wx((4,))
-    hop(2, 0)
-    hop(1, 2)
-    y_arrive_forward(0, 5)
-    w1_ready(4)
-    mat1(4)
-    start_wx((5,))
-    hop(2, 1)
-    w1_ready(5)
-    mat1(5)
-    hop(1, 3)
-    y_arrive_forward(1, 0)
-    hop(2, 2)
-    y_arrive_forward(1, 1)
-    hop(1, 4)
-    w2_ready(0)
-    mat2(pair_a, 0)
-    mat2x(0)
-    mat2x(1)
-    hop(2, 3)
-    y_arrive_forward(1, 2)
-    w2_ready(1)
-    mat2(pair_a, 1)
-    mat2x(2)
-    mat2x(3)
-    hop(1, 5)
-    y_arrive_forward(1, 3)
-    w2_ready(2)
-    mat2(pair_a, 2)
-    mat2x(4)
-    hop(2, 4)
-    mat2x(5)
-    px_start()
-    hop(2, 5)
-    y_arrive_forward(1, 4)
-    px_finish()
-    w2_ready(3)
-    mat2(pair_a, 3)
-    hop(3, 0)
-    mat2(pair_b, 0)
-    y_arrive_forward(1, 5)
-    hop(3, 1)
-    mat2(pair_b, 1)
-    w2_ready(4)
-    mat2(pair_a, 4)
-    hop(3, 2)
-    mat2(pair_b, 2)
-    hop(3, 3)
-    mat2(pair_b, 3)
-    w2_ready(5)
-    mat2(pair_a, 5)
-    hop(3, 4)
-    mat2(pair_b, 4)
-    hop(3, 5)
-    mat2(pair_b, 5)
+    events = dict(
+        own=own_x_send, x=xhop, xd=x_done, g=gamma_done, ln=norm, y=y_arrive_forward, w=start_w,
+        wx=lambda j: start_wx((j,)), wy=start_wx2, p=w1_ready, q=w2_local, r=w2_remote, f=mat1, h=hop,
+        a=functools.partial(mat2, pair_a), b=functools.partial(mat2, pair_b), c=mat2x, d=mat2y,
+        ps=px_start, pf=px_finish)
+    for code in ORDER:
+        name, *index = code.split("_")
+        events[name](*map(int, index))
     def fin_desc(m):
         return rcopy(acc.at[pl.ds(m * hrow + (1 - c) * mbt, mbt), :], part.at[pl.ds(m * mbt, mbt), :],
                      fs.at[m], fr.at[m], partner)
@@ -524,21 +499,16 @@
             for m in range(2):
                 x_dn(zz, m).wait_send()
 
-        @pl.when(jnp.logical_and(zz <= z, goes_up(zz)))
-        def _():
-            def d(j, _):
+        for j in range(NCHUNK):
+            @pl.when(jnp.logical_and(zz <= z, goes_up(zz, j)))
+            def _():
                 for m in range(2):
                     h_up(zz, j, m).wait_send()
-                return 0
-            lax.fori_loop(0, NCHUNK, d, 0)
-
-        @pl.when(jnp.logical_and(zz >= z, goes_dn(zz)))
-        def _():
-            def d(j, _):
+
+            @pl.when(jnp.logical_and(zz >= z, goes_dn(zz, j)))
+            def _():
                 for m in range(2):
                     h_dn(zz, j, m).wait_send()
-                return 0
-            lax.fori_loop(0, NCHUNK, d, 0)
         return 0
     lax.fori_loop(0, 4, drain_z, 0)
 
@@ -549,6 +519,11 @@
                 wx_desc(j, ct).wait_send()
             return 0
         lax.fori_loop(0, NCHUNK, d, 0)
+
+    @pl.when(end)
+    def _():
+        for j in EXTRA:
+            wx2_desc(j, False).wait_send()
 
     @pl.when(inner)
     def _():
@@ -579,9 +554,10 @@
                 jax.ShapeDtypeStruct((4, NCHUNK, nc, dblk), bf16),
                 jax.ShapeDtypeStruct((4, NCHUNK, 2 * tok, nc), bf16),
                 jax.ShapeDtypeStruct((NCHUNK, nc, dblk), bf16),
+                jax.ShapeDtypeStruct((max(len(EXTRA), 1), nc, dblk), bf16),
             ),
             in_specs=[anyspec] * 4,
-            out_specs=(pl.BlockSpec(memory_space=pltpu.VMEM), anyspec, anyspec, anyspec, anyspec),
+            out_specs=(pl.BlockSpec(memory_space=pltpu.VMEM), anyspec, anyspec, anyspec, anyspec, anyspec),
             scratch_shapes=[
                 pltpu.VMEM((4, 2 * tok, dblk), bf16),
                 pltpu.VMEM((2 * tok, 4 * dblk), bf16),
@@ -600,7 +576,8 @@
                 dma((2, NCHUNK)), dma((2, NCHUNK)),
                 dma((4, 2)), dma((4, 2)), dma((4, 2)), dma((4, 2)), dma((4, 2)), dma((3,)), dma((4,)),
                 dma((4, NCHUNK, 2)), dma((4, NCHUNK, 2)), dma((4, NCHUNK, 2)), dma((2,)), dma((2,)),
-                dma((NCHUNK, 2)), dma((NCHUNK,)), dma((2,)), dma((2,)), dma, dma,
+                dma((NCHUNK, 2)), dma((NCHUNK,)), dma((max(len(EXTRA), 1),)), dma((max(len(EXTRA), 1),)),
+                dma((2,)), dma((2,)), dma, dma,
                 dma((4,)), dma((2, 4)), dma((1,)), dma((2, 2)),
             ],
             compiler_params=pltpu.CompilerParams(

time: 519 us -> 475 us (0.915)
  the two profiles are of different devices: /device:TPU:30 before, /device:TPU:0 now
where the time goes in v3:
time: 475 us; the launch traced here: 474 us
  Pallas kernels  470 us (99%)
    pallas_call x1, Pallas kernels, per_device(): pl.pallas_call(_kernel, out_shape=(jax.ShapeDtypeStruct((tok, dblk), bf16...  470 us

profile of v3, /device:TPU:0, one launch (start us, length us, event | category | flops | bytes accessed | tf_op | source)
XLA Modules:
  0.0 474.3 jit_solution(4873432733913622840)
XLA Ops:
  0.0 1.3 broadcast_in_dim.2.gamma_ref
  1.3 470.4 %mlp.1 = (bf16[512,1536]{1,0:T(8,128)(2,1)}, bf16[6,4,1536,512]{3,2,1,0:T(8,128)(2,1)}, bf16[4,6,512,1536]{3,2,1,0:T(8,128)(2,1)}, bf16[4,6,1024,512]{3,2,1,0:T(...) custom-call(bf16[512,1536]{1,0:T(8,128)(2,1)} %bitcast.3, ...), custom_call_target="tpu_custom_call" | custom-call | tf_op jit(solution)/shard_map/mlp/pallas_call | solution.py:549
  471.7 2.7 copy.6

commit v4 on v3

--- a/solution.py
+++ b/solution.py
@@ -13,17 +13,18 @@
 LN_ROWS = 16
 EXTRA = ()
 ORDER = (
-    "own_1", "wx_1", "g", "y_0_0", "wx_0", "x_1_0", "x_2_0", "w_1", "x_1_1", "x_3_0", "p_0", "y_0_1",
-    "xd_0", "ln_0", "x_2_1", "f_0_0_1", "x_3_1", "y_0_2", "xd_1", "ln_1", "f_0_1_2", "p_1", "f_1",
-    "h_1_0_0", "y_0_3", "h_1_0_1", "p_2", "h_2_0_0", "f_2", "h_1_1_0", "wx_3", "h_2_0_1", "y_0_4",
-    "h_1_2_0", "h_1_1_1", "h_1_2_1", "p_3", "f_3", "y_0_5", "q_4", "q_1", "q_3", "p_4", "h_2_1_0",
-    "h_3_0_1", "h_2_2_0", "f_4", "y_1_0", "c_0", "wx_2", "q_0", "h_3_0_0", "q_2", "h_1_3_0", "h_2_1_1",
-    "h_1_3_1", "h_3_1_0", "c_1", "h_1_4_0", "p_5", "f_5", "h_1_4_1", "y_1_1", "h_3_1_1", "r_0",
-    "h_2_3_1", "h_2_3_0", "wx_4", "a_0", "h_3_2_0", "h_2_2_1", "h_2_4_0", "y_1_2", "h_1_5_1", "wx_5",
-    "h_1_5_0", "c_2", "y_1_3", "c_4", "h_3_3_0", "h_3_3_1", "b_0", "h_2_5_1", "r_2", "r_1", "h_3_2_1",
-    "c_3", "a_2", "a_1", "h_2_5_0", "b_2", "h_2_4_1", "c_5", "q_5", "r_3", "y_1_4", "h_3_4_0",
-    "h_3_4_1", "ps", "pf", "a_3", "y_1_5", "r_4", "b_3", "b_4", "h_3_5_1", "a_4", "b_1", "h_3_5_0",
-    "a_5", "r_5", "b_5",
+    "own_1", "wx_1", "y_0_0", "x_1_0", "x_2_0", "wx_0", "x_1_1", "y_0_1", "x_3_0", "g", "xd_0", "ln_0",
+    "x_2_1", "p_0", "f_0_0_1", "y_0_2", "x_3_1", "xd_1", "ln_1", "f_0_1_2", "w_1", "p_1", "f_1",
+    "h_1_0_0", "h_1_0_1", "p_2", "y_0_3", "h_1_1_0", "c_0", "e_0_0", "e_0_1", "f_2", "e_1_0", "h_2_0_0",
+    "h_1_1_1", "y_0_4", "e_1_1", "h_1_2_0", "q_3", "h_2_0_1", "e_2_0", "wx_3", "q_2", "h_2_1_0",
+    "e_2_1", "p_3", "h_1_2_1", "y_0_5", "f_3", "p_4", "f_4", "h_2_1_1", "h_3_1_0", "h_2_2_0", "e_3_0",
+    "h_2_2_1", "e_3_1", "y_1_0", "wx_2", "h_1_3_1", "h_1_3_0", "h_3_0_1", "p_5", "y_1_1", "h_1_4_1",
+    "h_1_4_0", "e_4_0", "f_5", "h_3_1_1", "h_2_3_0", "e_4_1", "r_0", "y_1_2", "h_3_0_0", "wx_4", "c_2",
+    "h_2_4_0", "r_1", "h_2_3_1", "b_1", "wx_5", "q_0", "c_3", "c_1", "h_3_2_1", "h_3_2_0", "a_2",
+    "e_5_1", "e_5_0", "b_0", "h_1_5_1", "h_3_3_0", "r_2", "y_1_3", "h_1_5_0", "a_0", "q_1", "h_3_3_1",
+    "h_2_4_1", "c_4", "h_2_5_1", "a_1", "q_4", "a_3", "h_2_5_0", "b_2", "y_1_4", "c_5", "q_5",
+    "h_3_4_1", "ps", "r_3", "h_3_5_1", "pf", "h_3_4_0", "h_3_5_0", "b_3", "r_4", "y_1_5", "b_4", "a_5",
+    "a_4", "r_5", "b_5",
 )
 
 
@@ -307,9 +308,10 @@
             def _():
                 h_dn(z, j, m).start()
 
-    def hop(h, j, *ms):
+    def hop(h, j, *ms, from_end=False):
+        first = h == 1
         for m in ms:
-            @pl.when(jnp.logical_and(z >= h, jnp.logical_not(jnp.logical_and(z == 3, not_taken(3, z - h, j)))))
+            @pl.when(jnp.logical_and(jnp.logical_and(z >= h, ((z == 1) == from_end) if first else True), jnp.logical_not(jnp.logical_and(z == 3, not_taken(3, z - h, j)))))
             def _():
                 h_up(z - h, j, m).wait_recv()
 
@@ -317,7 +319,7 @@
                 def _():
                     h_up(z - h, j, m).start()
 
-            @pl.when(jnp.logical_and(z + h <= 3, jnp.logical_not(jnp.logical_and(z == 0, not_taken(0, z + h, j)))))
+            @pl.when(jnp.logical_and(jnp.logical_and(z + h <= 3, ((z == 2) == from_end) if first else True), jnp.logical_not(jnp.logical_and(z == 0, not_taken(0, z + h, j)))))
             def _():
                 h_dn(z + h, j, m).wait_recv()
 
@@ -441,6 +443,7 @@
     events = dict(
         own=own_x_send, x=xhop, xd=x_done, g=gamma_done, ln=norm, y=y_arrive_forward, w=start_w,
         wx=lambda j: start_wx((j,)), wy=start_wx2, p=w1_ready, q=w2_local, r=w2_remote, f=mat1, h=hop,
+        e=lambda j, m: hop(1, j, m, from_end=True),
         a=functools.partial(mat2, pair_a), b=functools.partial(mat2, pair_b), c=mat2x, d=mat2y,
         ps=px_start, pf=px_finish)
     for code in ORDER:

time: 475 us -> 470 us (0.989)
  Pallas kernels: 470 us -> 465 us
    pallas_call x1, Pallas kernels: 470 us -> 465 us  [per_device(): pl.pallas_call(_kernel, out_shape=(jax.ShapeDtypeStruct((tok, dblk), bf16...]
where the time goes in v4:
time: 470 us; the launch traced here: 469 us
  Pallas kernels  465 us (99%)
    pallas_call x1, Pallas kernels, per_device(): pl.pallas_call(_kernel, out_shape=(jax.ShapeDtypeStruct((tok, dblk), bf16...  465 us

profile of v4, /device:TPU:0, one launch (start us, length us, event | category | flops | bytes accessed | tf_op | source)
XLA Modules:
  0.0 468.7 jit_solution(2811979758278009570)
XLA Ops:
  0.0 1.3 broadcast_in_dim.2.gamma_ref
  1.3 464.7 %mlp.1 = (bf16[512,1536]{1,0:T(8,128)(2,1)}, bf16[6,4,1536,512]{3,2,1,0:T(8,128)(2,1)}, bf16[4,6,512,1536]{3,2,1,0:T(8,128)(2,1)}, bf16[4,6,1024,512]{3,2,1,0:T(...) custom-call(bf16[512,1536]{1,0:T(8,128)(2,1)} %bitcast.3, ...), custom_call_target="tpu_custom_call" | custom-call | tf_op jit(solution)/shard_map/mlp/pallas_call | solution.py:552
  466.0 2.7 copy.6
